TPU v7x, 32 devices: a whole 2x2x4 slice. The times are simulated.
32 devices in a mesh: island: 4 (over y, core), shard: 8 (over z, x).
Axes of the slice: x: 2, y: 2, z: 4, core: 2. Of those that a mesh axis runs over, the one named last changes fastest.
Arguments:
- pseudo_grad: float32 [4, 2048, 4096], P('island', 'shard'), may hold values from -6 to 6
- error_buffer: float32 [4, 2048, 4096], P('island', 'shard'), may hold values from -6 to 6
- momentum: float32 [2048, 4096], P('shard'), may hold values from -4 to 4
- weights: bfloat16 [2048, 4096], P('shard'), may hold values from -6 to 6
- warm_basis: float32 [2048, 64], P('shard'), may hold values from -6 to 6
Outputs:
- new_error: float32 [4, 2048, 4096], P('island', 'shard')
- new_momentum: float32 [2048, 4096], P('shard')
- new_weights: bfloat16 [2048, 4096], P('shard')
- new_basis: float32 [2048, 64], P('shard')
All inputs are finite; a program needn't handle non-finite values.
Results may differ from a plain program's by a relative error of at most 0.001.
Values sent between devices are 32-bit elements; how exact they have to be, the bound alone decides.
A program may use at most 128 MiB of HBM per device.

v0:
```python
import jax
import jax.numpy as jnp
from jax import lax
from jax.sharding import PartitionSpec as P

ITERS = 2
HIGH = lax.Precision.HIGHEST
outer_beta = 0.9
outer_rate = 0.7


def orthonormal(factor_rows):
    gram_matrix = jnp.dot(factor_rows, factor_rows.T, precision=HIGH)
    lower_factor = jnp.linalg.cholesky(gram_matrix)
    return lax.linalg.triangular_solve(lower_factor, factor_rows, left_side=True, lower=True)


def on_device(pseudo_grad, error_buffer, momentum, weights, warm_basis):
    merged = (pseudo_grad + error_buffer)[0]
    basis_now = warm_basis
    for iteration in range(ITERS):
        partial_value = lax.dot_general(basis_now, merged, (((0,), (0,)), ((), ())), precision=HIGH)
        factor_rows = orthonormal(lax.psum(partial_value, ("island", "shard")))
        local_proj = lax.dot_general(merged, factor_rows, (((1,), (1,)), ((), ())), precision=HIGH)
        basis_now = lax.psum(local_proj, "island")
    new_error = merged - jnp.dot(local_proj, factor_rows, precision=HIGH)
    update = jnp.dot(basis_now / lax.axis_size("island"), factor_rows, precision=HIGH)
    new_momentum = outer_beta * momentum + update
    stepped = weights.astype(jnp.float32) - outer_rate * (update + outer_beta * new_momentum)
    return (new_error[None], new_momentum, stepped.astype(jnp.bfloat16), basis_now)


def solution(mesh):
    in_specs = (
        P("island", "shard", None),
        P("island", "shard", None),
        P("shard", None),
        P("shard", None),
        P("shard", None),
    )
    out_specs = (P("island", "shard", None), P("shard", None), P("shard", None), P("shard", None))
    return jax.shard_map(
        on_device, mesh=mesh, in_specs=in_specs, out_specs=out_specs, check_vma=False
    )
```

profile of v0, /device:TPU:0, one launch (start us, length us, event | category | flops | bytes accessed | tf_op | source)
XLA Modules:
  0.0 420.1 jit_solution(8857783116008560494)
XLA Ops:
  7.2 0.0 copy-start
  7.2 0.0 all-reduce.5.cloned.1.call-start
  7.2 3.9 add.25
  11.2 0.0 copy-start.1
  11.2 2.0 copy-done.1
  13.2 0.0 copy-done
  13.2 3.8 convolution_bitcast_fusion
  17.0 0.0 all-reduce.5.cloned.1.call-update
  17.0 0.0 all-reduce.7.cloned.1.call-start
  17.1 133.6 %all-reduce.5.cloned.1.call-done = f32[64,4096]{1,0:T(8,128)} async-done(((f32[64,4096]{1,0:T(8,128)}), f32[64,4096]{1,0:T(8,128)}) %all-reduce.5.cloned.1.call-update) | async-done | bytes 1048592 | tf_op jit(solution)/shard_map/psum | solution.py:23
  150.7 2.5 fusion.22
  153.3 0.1 copy.9
  153.3 5.8 %cholesky.44 = f32[64,64]{1,0:T(8,128)S(1)} custom-call(f32[64,64]{1,0:T(8,128)S(1)} %fusion.17), custom_call_target="Cholesky" | custom-call | tf_op jit(solution)/shard_map/jit(cholesky)/cholesky | solution.py:14
  159.2 0.6 compare_reduce_fusion.1
  159.9 0.7 fusion.10
  160.5 4.9 %custom-call.6 = f32[1,64,64]{1,2,0:T(8,128)S(1)} custom-call(f32[1,64,64]{2,1,0:T(8,128)S(1)} %fusion.10), custom_call_target="InvertDiagBlocksLowerTriangular" | custom-call | tf_op jit(solution)/shard_map/triangular_solve/custom-call.0 | solution.py:15
  165.4 2.3 fusion.15
  167.7 5.8 %fusion.5 = f32[256,64]{1,0:T(8,128)} fusion(f32[64,4096]{1,0:T(8,128)S(1)} %fusion.15, f32[1,256,4096]{2,1,0:T(8,128)} %copy-done.1), kind=kOutput, calls=%fused_computation.7 | convolution fusion | flops 805306368 | bytes 5308416 | tf_op jit(solution)/shard_map/dot_general | solution.py:24
  173.5 0.0 all-reduce.7.cloned.1.call-update
  173.6 0.2 all-reduce.9.cloned.1.call-start
  173.8 30.7 %all-reduce.7.cloned.1.call-done = f32[256,64]{1,0:T(8,128)} async-done(((f32[256,64]{1,0:T(8,128)}), f32[256,64]{1,0:T(8,128)}) %all-reduce.7.cloned.1.call-update) | async-done | bytes 65552 | tf_op jit(solution)/shard_map/psum | solution.py:25
  204.4 5.9 %fusion.3 = f32[64,4096]{1,0:T(8,128)} fusion(f32[256,64]{1,0:T(8,128)} %all-reduce.7.cloned.1.call-done, f32[1,256,4096]{2,1,0:T(8,128)} %copy-done.1), kind=kOutput, calls=%fused_computation.5 | convolution fusion | flops 805306368 | bytes 5308416 | tf_op jit(solution)/shard_map/dot_general | solution.py:22
  210.3 0.0 all-reduce.9.cloned.1.call-update
  210.3 130.9 %all-reduce.9.cloned.1.call-done = f32[64,4096]{1,0:T(8,128)} async-done(((f32[64,4096]{1,0:T(8,128)}), f32[64,4096]{1,0:T(8,128)}) %all-reduce.9.cloned.1.call-update) | async-done | bytes 1048592 | tf_op jit(solution)/shard_map/psum | solution.py:23
  341.2 2.5 fusion.23
  343.8 0.1 copy.10
  343.9 5.8 %cholesky.55 = f32[64,64]{1,0:T(8,128)S(1)} custom-call(f32[64,64]{1,0:T(8,128)S(1)} %fusion.14), custom_call_target="Cholesky" | custom-call | tf_op jit(solution)/shard_map/jit(cholesky)/cholesky | solution.py:14
  349.7 0.6 compare_reduce_fusion
  350.4 0.7 fusion.11
  351.1 4.9 %custom-call.7 = f32[1,64,64]{1,2,0:T(8,128)S(1)} custom-call(f32[1,64,64]{2,1,0:T(8,128)S(1)} %fusion.11), custom_call_target="InvertDiagBlocksLowerTriangular" | custom-call | tf_op jit(solution)/shard_map/triangular_solve/custom-call.0 | solution.py:15
  355.9 2.3 fusion.12
  358.2 6.1 %fusion.1 = f32[256,64]{0,1:T(8,128)S(1)} fusion(f32[64,4096]{1,0:T(8,128)S(1)} %fusion.12, f32[1,256,4096]{2,1,0:T(8,128)} %copy-done.1), kind=kOutput, calls=%fused_computation.3 | convolution fusion | flops 805306368 | bytes 5308416 | tf_op jit(solution)/shard_map/dot_general | solution.py:24
  364.3 0.0 copy-start.3
  364.3 0.0 copy-start.2
  364.4 6.8 %fusion = f32[1,256,4096]{2,1,0:T(8,128)} fusion(f32[256,64]{0,1:T(8,128)S(1)} %fusion.1, f32[64,4096]{1,0:T(8,128)S(1)} %fusion.12, f32[1,256,4096]{2,1,0:T(8,128)} %copy-done.1), kind=kOutput, calls=%fused_computation.1 | convolution fusion | flops 806354944 | bytes 9502720 | tf_op jit(solution)/shard_map/dot_general | solution.py:26
  371.1 0.0 copy-done.3
  371.1 0.0 all-reduce.11.cloned.1.call-start
  371.1 0.6 all-reduce.11.cloned.1.call-update
  371.7 33.3 %all-reduce.11.cloned.1.call-done = f32[256,64]{0,1:T(8,128)} async-done(((f32[256,64]{0,1:T(8,128)}), f32[256,64]{0,1:T(8,128)}) %all-reduce.11.cloned.1.call-update) | async-done | bytes 65552 | tf_op jit(solution)/shard_map/psum | solution.py:25
  405.0 0.0 copy-done.2
  405.0 0.0 copy-start.4
  405.0 7.9 %subtract_convert_fusion = (bf16[256,4096]{1,0:T(8,128)(2,1)}, f32[256,4096]{1,0:T(8,128)}) fusion(bf16[256,4096]{1,0:T(8,128)(2,1)S(1)} %copy-done.2, f32[256,4096]{1,0:T(8,128)} %param.10, f32[64,4096]{1,0:T(8,128)S(1)} %fusion.12, f32[256,64]{0,1:T(8,128)} %all-reduce.11.cloned.1.call-done), kind=kOutput, calls=%fused_computation.10 | convolution fusion | flops 813711360 | bytes 13697024 | tf_op jit(solution)/shard_map/dot_general | solution.py:27
  412.9 0.0 copy-done.4
  412.9 0.6 copy.15
  (4 shorter events, 0.1 us)
Async XLA Ops:
  7.2 6.0 %copy-start = (f32[256,64]{0,1:T(8,128)S(1)}, f32[256,64]{0,1:T(8,128)}, u32[]{:S(2)}) copy-start(f32[256,64]{0,1:T(8,128)} %param.12) | copy-start | bytes 196612
  7.2 143.5 %all-reduce.5.cloned.1.call-start = ((), (), s32[]{:S(2)}) async-start(), calls=%async_computation | async-start | bytes 2097152 | tf_op jit(solution)/shard_map/psum | solution.py:23
  11.2 2.0 copy-start.1
  17.0 187.4 %all-reduce.7.cloned.1.call-start = ((), (), s32[]{:S(2)}) async-start(), calls=%async_computation.1 | async-start | bytes 262144 | tf_op jit(solution)/shard_map/psum | solution.py:25
  173.6 167.7 %all-reduce.9.cloned.1.call-start = ((), (), s32[]{:S(2)}) async-start(), calls=%async_computation.2 | async-start | bytes 2097152 | tf_op jit(solution)/shard_map/psum | solution.py:23
  364.3 6.8 %copy-start.3 = (f32[256,64]{0,1:T(8,128)}, f32[256,64]{0,1:T(8,128)S(1)}, u32[]{:S(2)}) copy-start(f32[256,64]{0,1:T(8,128)S(1)} %fusion.1) | copy-start | bytes 196612
  364.3 40.7 %copy-start.2 = (bf16[256,4096]{1,0:T(8,128)(2,1)S(1)}, bf16[256,4096]{1,0:T(8,128)(2,1)}, u32[]{:S(2)}) copy-start(bf16[256,4096]{1,0:T(8,128)(2,1)} %param.11) | copy-start | bytes 6291460
  371.1 33.9 %all-reduce.11.cloned.1.call-start = ((), (), s32[]{:S(2)}) async-start(), calls=%async_computation.3 | async-start | bytes 131072 | tf_op jit(solution)/shard_map/psum | solution.py:25
  405.0 7.9 %copy-start.4 = (f32[256,64]{0,1:T(8,128)S(1)}, f32[256,64]{0,1:T(8,128)}, u32[]{:S(2)}) copy-start(f32[256,64]{0,1:T(8,128)} %all-reduce.11.cloned.1.call-done) | copy-start | bytes 196612
Sparse Core Ops, SparseCore 0:
  17.2 133.5 all-reduce.4
  173.7 30.7 all-reduce.6
  210.5 130.7 all-reduce.8
  374.5 30.4 all-reduce.10
where the time goes:
time: 420 us
  waiting for transfers between devices  329 us (78%)
  matrix products  45.8 us (11%)
  other arithmetic  28.1 us (7%)
  between operations  13.9 us (3%)
    psum x2, waiting for transfers between devices, on_device(): factor_rows = orthonormal(lax.psum(partial_value, ('island', 'shard')))  265 us
    psum x2, waiting for transfers between devices, on_device(): basis_now = lax.psum(local_proj, 'island')  64 us
    another operation x6, other arithmetic, orthonormal(): lower_factor = jnp.linalg.cholesky(gram_matrix)  13 us
    dot_general x2, matrix products, on_device(): lax.dot_general(merged, factor_rows, (((1,), (1,)), ((), ())), precision=...  11.9 us
    another operation x4, other arithmetic, orthonormal(): lax.linalg.triangular_solve(lower_factor, factor_rows, left_side=True, lo...  11.1 us
    dot_general x2, matrix products, on_device(): lax.dot_general(basis_now, merged, (((0,), (0,)), ((), ())), precision=HIGH)  9.69 us
  transfers between devices with their start and end apart: 4, of which 4 were waited for; matrix products, arithmetic and copies ran while one was open for 0% of the time, Pallas kernels for 0%

commit v1 on v0

--- a/solution.py
+++ b/solution.py
@@ -22,7 +22,8 @@
         partial_value = lax.dot_general(basis_now, merged, (((0,), (0,)), ((), ())), precision=HIGH)
         factor_rows = orthonormal(lax.psum(partial_value, ("island", "shard")))
         local_proj = lax.dot_general(merged, factor_rows, (((1,), (1,)), ((), ())), precision=HIGH)
-        basis_now = lax.psum(local_proj, "island")
+        store_classes = lambda mine, along_axis: jnp.sum(lax.all_gather(mine, along_axis), axis=0)
+        basis_now = store_classes(local_proj, "island")
     new_error = merged - jnp.dot(local_proj, factor_rows, precision=HIGH)
     update = jnp.dot(basis_now / lax.axis_size("island"), factor_rows, precision=HIGH)
     new_momentum = outer_beta * momentum + update

time: 420 us -> 367 us (0.87)
  waiting for transfers between devices: 329 us -> 264 us
  blocking collectives: 0 us -> 12.4 us
    psum x2 -> x0, waiting for transfers between devices: 64 us -> none  [on_device(): basis_now = lax.psum(local_proj, 'island')]
    all_gather x0 -> x2, blocking collectives: none -> 12.4 us  [on_device(): lax.all_gather(mine, along_axis)]
  transfers between devices with their start and end apart: 4 -> 2, of which waited for: 4 -> 2; matrix products, arithmetic and copies ran while one was open for 0% -> 0% of each run, Pallas kernels for 0% -> 0%
where the time goes in v1:
time: 367 us
  waiting for transfers between devices  264 us (72%)
  matrix products  44.5 us (12%)
  other arithmetic  28.4 us (8%)
  between operations  14.2 us (4%)
  blocking collectives  12.4 us (3%)
    psum x2, waiting for transfers between devices, on_device(): factor_rows = orthonormal(lax.psum(partial_value, ('island', 'shard')))  264 us
    another operation x6, other arithmetic, orthonormal(): lower_factor = jnp.linalg.cholesky(gram_matrix)  13 us
    all_gather x2, blocking collectives, on_device(): lax.all_gather(mine, along_axis)  12.4 us
    dot_general x2, matrix products, on_device(): lax.dot_general(merged, factor_rows, (((1,), (1,)), ((), ())), precision=...  12.2 us
    another operation x4, other arithmetic, orthonormal(): lax.linalg.triangular_solve(lower_factor, factor_rows, left_side=True, lo...  11.1 us
    dot_general x2, matrix products, on_device(): lax.dot_general(basis_now, merged, (((0,), (0,)), ((), ())), precision=HIGH)  9.6 us
    dot_general x1, matrix products, on_device(): jnp.dot(basis_now / lax.axis_size('island'), factor_rows, precision=HIGH)  7.85 us
  transfers between devices with their start and end apart: 2, of which 2 were waited for; matrix products, arithmetic and copies ran while one was open for 0% of the time, Pallas kernels for 0%

profile of v1, /device:TPU:0, one launch (start us, length us, event | category | flops | bytes accessed | tf_op | source)
XLA Modules:
  0.0 366.5 jit_solution(98535912545339685)
XLA Ops:
  7.2 0.0 copy-start
  7.2 0.0 all-reduce.3.cloned.1.call-start
  7.2 3.9 %add.21 = f32[1,256,4096]{2,1,0:T(8,128)S(1)} add(f32[1,256,4096]{2,1,0:T(8,128)} %param.8, f32[1,256,4096]{2,1,0:T(8,128)} %param.9) | non-fusion elementwise | flops 1048576 | bytes 12582912 | tf_op jit(solution)/shard_map/add | solution.py:19
  11.2 0.0 copy-start.1
  11.2 2.0 copy-done.1
  13.2 0.0 copy-done
  13.2 3.8 %convolution_bitcast_fusion = f32[64,4096]{1,0:T(8,128)} fusion(f32[256,64]{0,1:T(8,128)S(1)} %copy-done, f32[1,256,4096]{2,1,0:T(8,128)S(1)} %add.21), kind=kOutput, calls=%fused_computation.2 | convolution fusion | flops 805306368 | bytes 5308416 | tf_op jit(solution)/shard_map/dot_general | solution.py:22
  17.0 0.0 all-reduce.3.cloned.1.call-update
  17.0 0.0 all-reduce.5.cloned.1.call-start
  17.1 133.6 %all-reduce.3.cloned.1.call-done = f32[64,4096]{1,0:T(8,128)} async-done(((f32[64,4096]{1,0:T(8,128)}), f32[64,4096]{1,0:T(8,128)}) %all-reduce.3.cloned.1.call-update) | async-done | bytes 1048592 | tf_op jit(solution)/shard_map/psum | solution.py:23
  150.7 2.5 fusion.22
  153.3 0.1 copy.11
  153.3 5.8 %cholesky.44 = f32[64,64]{1,0:T(8,128)S(1)} custom-call(f32[64,64]{1,0:T(8,128)S(1)} %fusion.17), custom_call_target="Cholesky" | custom-call | tf_op jit(solution)/shard_map/jit(cholesky)/cholesky | solution.py:14
  159.2 0.6 compare_reduce_fusion.1
  159.9 0.7 fusion.10
  160.5 4.9 %custom-call.6 = f32[1,64,64]{1,2,0:T(8,128)S(1)} custom-call(f32[1,64,64]{2,1,0:T(8,128)S(1)} %fusion.10), custom_call_target="InvertDiagBlocksLowerTriangular" | custom-call | tf_op jit(solution)/shard_map/triangular_solve/custom-call.0 | solution.py:15
  165.4 2.3 fusion.15
  167.7 6.1 %fusion.5 = f32[256,64]{0,1:T(8,128)S(1)} fusion(f32[64,4096]{1,0:T(8,128)S(1)} %fusion.15, f32[1,256,4096]{2,1,0:T(8,128)} %copy-done.1), kind=kOutput, calls=%fused_computation.7 | convolution fusion | flops 805306368 | bytes 5308416 | tf_op jit(solution)/shard_map/dot_general | solution.py:24
  173.8 6.0 %all-gather = f32[1024,64]{0,1:T(8,128)S(1)} all-gather(f32[256,64]{0,1:T(8,128)S(1)} %fusion.5), channel_id=2, replica_groups=mesh['island'=4,'shard'=8] {'island'}, dimensions={0}, use_global_device_ids=true | all-gather | bytes 327680 | tf_op jit(solution)/shard_map/all_gather | solution.py:25
  179.8 0.1 reshape.21
  179.9 0.2 reduce_sum.18
  180.1 5.8 %fusion.3 = f32[64,4096]{1,0:T(8,128)} fusion(f32[256,64]{0,1:T(8,128)S(1)} %reduce_sum.18, f32[1,256,4096]{2,1,0:T(8,128)} %copy-done.1), kind=kOutput, calls=%fused_computation.5 | convolution fusion | flops 805306368 | bytes 5308416 | tf_op jit(solution)/shard_map/dot_general | solution.py:22
  185.9 0.0 all-reduce.5.cloned.1.call-update
  185.9 129.9 %all-reduce.5.cloned.1.call-done = f32[64,4096]{1,0:T(8,128)} async-done(((f32[64,4096]{1,0:T(8,128)}), f32[64,4096]{1,0:T(8,128)}) %all-reduce.5.cloned.1.call-update) | async-done | bytes 1048592 | tf_op jit(solution)/shard_map/psum | solution.py:23
  315.8 2.5 fusion.23
  318.3 0.1 copy.12
  318.4 5.8 %cholesky.55 = f32[64,64]{1,0:T(8,128)S(1)} custom-call(f32[64,64]{1,0:T(8,128)S(1)} %fusion.14), custom_call_target="Cholesky" | custom-call | tf_op jit(solution)/shard_map/jit(cholesky)/cholesky | solution.py:14
  324.3 0.6 compare_reduce_fusion
  324.9 0.7 fusion.11
  325.6 4.9 %custom-call.7 = f32[1,64,64]{1,2,0:T(8,128)S(1)} custom-call(f32[1,64,64]{2,1,0:T(8,128)S(1)} %fusion.11), custom_call_target="InvertDiagBlocksLowerTriangular" | custom-call | tf_op jit(solution)/shard_map/triangular_solve/custom-call.0 | solution.py:15
  330.5 0.0 copy-start.2
  330.5 2.4 fusion.12
  332.9 6.1 %fusion.1 = f32[256,64]{0,1:T(8,128)S(1)} fusion(f32[64,4096]{1,0:T(8,128)S(1)} %fusion.12, f32[1,256,4096]{2,1,0:T(8,128)} %copy-done.1), kind=kOutput, calls=%fused_computation.3 | convolution fusion | flops 805306368 | bytes 5308416 | tf_op jit(solution)/shard_map/dot_general | solution.py:24
  339.0 0.0 copy-done.2
  339.0 0.0 copy-start.3
  339.0 5.1 %fusion = f32[1,256,4096]{2,1,0:T(8,128)} fusion(f32[256,64]{0,1:T(8,128)S(1)} %fusion.1, f32[64,4096]{1,0:T(8,128)S(1)} %fusion.12, f32[1,256,4096]{2,1,0:T(8,128)S(1)} %copy-done.2), kind=kOutput, calls=%fused_computation.1 | convolution fusion | flops 806354944 | bytes 9502720 | tf_op jit(solution)/shard_map/dot_general | solution.py:27
  344.2 6.4 %all-gather.1 = f32[1024,64]{0,1:T(8,128)} all-gather(f32[256,64]{0,1:T(8,128)S(1)} %fusion.1), channel_id=3, replica_groups=mesh['island'=4,'shard'=8] {'island'}, dimensions={0}, use_global_device_ids=true | all-gather | bytes 327680 | tf_op jit(solution)/shard_map/all_gather | solution.py:25
  350.6 1.1 reshape.22
  351.7 0.2 reduce_sum.19
  351.8 0.0 copy-done.3
  351.8 0.0 copy-start.4
  351.8 7.8 %subtract_convert_fusion = (bf16[256,4096]{1,0:T(8,128)(2,1)}, f32[256,4096]{1,0:T(8,128)}) fusion(bf16[256,4096]{1,0:T(8,128)(2,1)S(1)} %copy-done.3, f32[256,4096]{1,0:T(8,128)} %param.10, f32[64,4096]{1,0:T(8,128)S(1)} %fusion.12, f32[256,64]{0,1:T(8,128)S(1)} %reduce_sum.19), kind=kOutput, calls=%fused_computation.10 | convolution fusion | flops 813711360 | bytes 13697024 | tf_op jit(solution)/shard_map/dot_general | solution.py:28
  359.7 0.0 copy-done.4
  (4 shorter events, 0.1 us)
Async XLA Ops:
  7.2 6.0 %copy-start = (f32[256,64]{0,1:T(8,128)S(1)}, f32[256,64]{0,1:T(8,128)}, u32[]{:S(2)}) copy-start(f32[256,64]{0,1:T(8,128)} %param.12) | copy-start | bytes 196612
  7.2 143.5 %all-reduce.3.cloned.1.call-start = ((), (), s32[]{:S(2)}) async-start(), calls=%async_computation | async-start | bytes 2097152 | tf_op jit(solution)/shard_map/psum | solution.py:23
  11.2 2.0 copy-start.1
  17.0 298.7 %all-reduce.5.cloned.1.call-start = ((), (), s32[]{:S(2)}) async-start(), calls=%async_computation.1 | async-start | bytes 2097152 | tf_op jit(solution)/shard_map/psum | solution.py:23
  330.5 8.5 %copy-start.2 = (f32[1,256,4096]{2,1,0:T(8,128)S(1)}, f32[1,256,4096]{2,1,0:T(8,128)}, u32[]{:S(2)}) copy-start(f32[1,256,4096]{2,1,0:T(8,128)} %copy-done.1) | copy-start | bytes 12582916
  339.0 12.8 %copy-start.3 = (bf16[256,4096]{1,0:T(8,128)(2,1)S(1)}, bf16[256,4096]{1,0:T(8,128)(2,1)}, u32[]{:S(2)}) copy-start(bf16[256,4096]{1,0:T(8,128)(2,1)} %param.11) | copy-start | bytes 6291460
  351.8 7.9 %copy-start.4 = (f32[256,64]{0,1:T(8,128)}, f32[256,64]{0,1:T(8,128)S(1)}, u32[]{:S(2)}) copy-start(f32[256,64]{0,1:T(8,128)S(1)} %reduce_sum.19) | copy-start | bytes 196612
Sparse Core Ops, SparseCore 0:
  17.2 133.5 all-reduce.2
  186.0 129.7 all-reduce.4
